TPU v7x, 32 devices: a whole 2x2x4 slice. The times are simulated.
32 devices in a mesh: iface: 8 (over z, y), dom: 4 (over x, core).
Axes of the slice: x: 2, y: 2, z: 4, core: 2. Of those that a mesh axis runs over, the one named last changes fastest.
Arguments:
- interface: float32 [131072], P(('iface', 'dom')), may hold values from -6 to 6
- previous_residual: float32 [131072], P(('iface', 'dom')), may hold values from -6 to 6
- previous_estimate: float32 [131072], P(('iface', 'dom')), may hold values from -6 to 6
- forcing: float32 [131072], P(('iface', 'dom')), may hold values from -60 to 60
- stiffness: float32 [131072], P(('iface', 'dom')), may hold values from 0.2 to 0.6
- history_residual: float32 [100, 131072], P(None, ('iface', 'dom')), may hold values from -40 to 40
- history_estimate: float32 [100, 131072], P(None, ('iface', 'dom')), may hold values from -6 to 6
Outputs:
- interface_next: float32 [131072], P(('iface', 'dom'))
- residual_last: float32 [131072], P(('iface', 'dom'))
All inputs are finite; a program needn't handle non-finite values.
Results may differ from a plain program's by a relative error of at most 0.0003.
Values sent between devices are 32-bit elements; how exact they have to be, the bound alone decides.
A program may use at most 64 MiB of HBM per device.

v0:
```python
import jax
import jax.numpy as jnp
from jax import lax
from jax.sharding import PartitionSpec as P

ITERS = 3
coupling = 0.25


def from_behind(value, axis, steps):
    count = lax.axis_size(axis)
    initial, last = (max(0, -steps), min(count, count - steps))
    return lax.ppermute(value, axis, [(source, source + steps) for source in range(initial, last)])


def solver_map(current, forcing, stiffness):
    from_left = from_behind(current[-1:], ("iface", "dom"), 1)
    from_right = from_behind(current[:1], ("iface", "dom"), -1)
    padded = jnp.concatenate([from_left, current, from_right], axis=0)
    return forcing + stiffness * jnp.tanh(current) + coupling * (padded[:-2] + padded[2:])


def shards(
    interface,
    previous_residual,
    previous_estimate,
    forcing,
    stiffness,
    history_residual,
    history_estimate,
):
    high = lax.Precision.HIGHEST
    current = interface
    hist_v = history_residual
    hist_w = history_estimate
    old_residual = previous_residual
    old_estimate = previous_estimate
    residual = previous_residual
    for iteration in range(ITERS):
        estimate = solver_map(current, forcing, stiffness)
        residual = estimate - current
        new_column = residual - old_residual
        hist_v = jnp.concatenate([hist_v, new_column[None, :]], axis=0)
        hist_w = jnp.concatenate([hist_w, (estimate - old_estimate)[None, :]], axis=0)
        gram_matrix, projection = lax.psum(
            (jnp.dot(hist_v, hist_v.T, precision=high), jnp.dot(hist_v, residual, precision=high)),
            ("iface", "dom"),
        )
        factor = jnp.linalg.cholesky(gram_matrix)
        coeffs = -jax.scipy.linalg.cho_solve((factor, True), projection)
        current = estimate + jnp.dot(coeffs, hist_w, precision=high)
        old_residual = residual
        old_estimate = estimate
    return (current, residual)


def solution(mesh):
    return jax.shard_map(
        shards,
        mesh=mesh,
        in_specs=(
            P(("iface", "dom")),
            P(("iface", "dom")),
            P(("iface", "dom")),
            P(("iface", "dom")),
            P(("iface", "dom")),
            P(None, ("iface", "dom")),
            P(None, ("iface", "dom")),
        ),
        out_specs=(P(("iface", "dom")), P(("iface", "dom"))),
        check_vma=False,
    )
```

profile of v0, /device:TPU:0, one launch (start us, length us, event | category | flops | bytes accessed | tf_op | source)
XLA Modules:
  0.0 240.4 jit_solution(12346703330274250481)
XLA Ops:
  0.6 0.0 copy-start
  0.6 1.4 fusion.75
  2.1 2.9 %collective-permute-start = (f32[1]{0:T(128)}, f32[1]{0:T(128)}, u32[]{:S(2)}, u32[]{:S(2)}) collective-permute-start(f32[1]{0:T(128)} %get-tuple-element.24), channel_id=1, source_target_pairs={{0,1},{1,2},{2,3},{3,4},{4,5},{5,6},{6,7},{7,8},{8,9},{9,10},{10,1... | collective-permute-start | bytes 20 | tf_op jit(solution)/shard_map/ppermute | solution.py:13
  5.0 1.3 collective-permute-start.1
  6.3 0.0 collective-permute-done
  6.3 3.4 %collective-permute-done.1 = f32[1]{0:T(128)} collective-permute-done((f32[1]{0:T(128)}, f32[1]{0:T(128)}, u32[]{:S(2)}, u32[]{:S(2)}) %collective-permute-start.1) | collective-permute-done | bytes 36 | tf_op jit(solution)/shard_map/ppermute | solution.py:13
  9.7 2.8 %fusion.70 = (f32[4096]{0:T(1024)}, f32[4096]{0:T(1024)S(1)}) fusion(f32[4096]{0:T(1024)} %param.9, f32[1]{0:T(128)} %collective-permute-done.1, f32[4096]{0:T(1024)} %param.7, f32[1]{0:T(128)} %collective-permute-done, f32[4096]{0:T(1024)} %param.10, f32[4096]{0:T(1024)} %param.11), kind=kLoop, calls=%fused_computation.102 | loop fusion | flops 32768 | bytes 98312 | tf_op jit(solution)/shard_map/sub | solution.py:44
  12.5 0.7 fusion.72
  13.3 0.0 copy-start.1
  13.3 3.6 %fusion.19 = f32[101,101]{0,1:T(8,128)S(1)} fusion(f32[1,4096]{1,0:T(1,128)S(1)} %bitcast.102, f32[100,4096]{1,0:T(8,128)} %param.12), kind=kOutput, calls=%fused_computation.22 | convolution fusion | flops 501813248 | bytes 1695588 | tf_op jit(solution)/shard_map/dot_general | solution.py:46
  16.9 0.0 copy-done.4
  17.0 1.4 fusion.29
  18.4 43.2 %all-reduce.2 = (f32[101,101]{0,1:T(8,128)S(1)}, f32[101]{0:T(128)S(1)}) all-reduce(f32[101,101]{0,1:T(8,128)S(1)} %fusion.19, f32[101]{0:T(128)S(1)} %fusion.29), channel_id=1, replica_groups=mesh['iface'=8,'dom'=4] {'iface','dom'}, use_global_device_ids=true, to_apply=%region_0.0 | all-reduce | flops 10302 | bytes 82416 | tf_op jit(solution)/shard_map/psum | solution.py:45
  61.6 0.1 copy.10
  61.7 0.6 fusion.42
  62.4 10.1 %cholesky.44 = f32[101,101]{1,0:T(8,128)S(1)} custom-call(f32[101,101]{1,0:T(8,128)} %fusion.42), custom_call_target="Cholesky" | custom-call | tf_op jit(solution)/shard_map/jit(cholesky)/cholesky | solution.py:49
  72.5 0.7 compare_reduce_fusion.2
  73.2 1.3 fusion.31
  74.5 8.5 %custom-call.30 = f32[1,101,101]{1,2,0:T(8,128)S(1)} custom-call(f32[1,101,101]{2,1,0:T(8,128)} %fusion.31), custom_call_target="InvertDiagBlocksLowerTriangular" | custom-call | tf_op jit(solution)/shard_map/jit(_cho_solve)/triangular_solve | solution.py:50
  83.1 0.0 copy-start.8
  83.1 0.2 convolution_bitcast_fusion.6
  83.2 0.2 fusion.23
  83.4 1.7 fusion
  85.1 0.7 fusion.74
  85.8 1.9 collective-permute-start.2
  87.6 1.5 collective-permute-start.3
  89.1 0.0 collective-permute-done.2
  89.1 3.7 %collective-permute-done.3 = f32[1]{0:T(128)} collective-permute-done((f32[1]{0:T(128)}, f32[1]{0:T(128)}, u32[]{:S(2)}, u32[]{:S(2)}) %collective-permute-start.3) | collective-permute-done | bytes 36 | tf_op jit(solution)/shard_map/ppermute | solution.py:13
  92.8 1.9 fusion.67
  94.7 0.0 copy-start.11
  94.7 2.1 fusion.21
  96.9 1.4 fusion.28
  98.3 42.2 %all-reduce.1 = (f32[102,102]{0,1:T(8,128)S(1)}, f32[102]{0:T(128)S(1)}) all-reduce(f32[102,102]{0,1:T(8,128)} %fusion.21, f32[102]{0:T(128)S(1)} %fusion.28), channel_id=1, replica_groups=mesh['iface'=8,'dom'=4] {'iface','dom'}, use_global_device_ids=true, to_apply=%region_4.5 | all-reduce | flops 10506 | bytes 84048 | tf_op jit(solution)/shard_map/psum | solution.py:45
  140.5 0.1 copy.12
  140.6 0.6 fusion.39
  141.3 10.2 %cholesky.86 = f32[102,102]{1,0:T(8,128)S(1)} custom-call(f32[102,102]{1,0:T(8,128)} %fusion.39), custom_call_target="Cholesky" | custom-call | tf_op jit(solution)/shard_map/jit(cholesky)/cholesky | solution.py:49
  151.5 0.7 compare_reduce_fusion.1
  152.1 1.3 fusion.32
  153.4 8.6 %custom-call.31 = f32[1,102,102]{1,2,0:T(8,128)S(1)} custom-call(f32[1,102,102]{2,1,0:T(8,128)} %fusion.32), custom_call_target="InvertDiagBlocksLowerTriangular" | custom-call | tf_op jit(solution)/shard_map/jit(_cho_solve)/triangular_solve | solution.py:50
  162.0 0.0 copy-start.12
  162.1 0.2 convolution_bitcast_fusion.4
  162.2 0.2 fusion.25
  162.4 1.7 fusion.4
  164.1 0.6 fusion.73
  164.7 1.8 collective-permute-start.4
  166.6 1.3 collective-permute-start.5
  167.8 0.0 collective-permute-done.4
  167.9 3.9 %collective-permute-done.5 = f32[1]{0:T(128)} collective-permute-done((f32[1]{0:T(128)}, f32[1]{0:T(128)}, u32[]{:S(2)}, u32[]{:S(2)}) %collective-permute-start.5) | collective-permute-done | bytes 36 | tf_op jit(solution)/shard_map/ppermute | solution.py:13
  171.8 1.9 fusion.64
  173.7 0.0 copy-start.16
  173.7 1.5 fusion.30
  175.2 0.0 copy-start.10
  175.3 1.4 convolution_bitcast_fusion.2
  176.7 42.2 %all-reduce = (f32[103,103]{0,1:T(8,128)S(1)}, f32[103]{0:T(128)S(1)}) all-reduce(f32[103,103]{0,1:T(8,128)S(1)} %fusion.30, f32[103]{0:T(128)S(1)} %convolution_bitcast_fusion.2), channel_id=1, replica_groups=mesh['iface'=8,'dom'=4] {'iface','dom'}, use_global_device_ids=true, to_apply=%region_8.9 | all-reduce | flops 10712 | bytes 85696 | tf_op jit(solution)/shard_map/psum | solution.py:45
  218.9 0.1 copy.14
  219.0 9.4 %cholesky.96 = f32[103,103]{1,0:T(8,128)S(1)} custom-call(f32[103,103]{1,0:T(8,128)S(1)} %fusion.36), custom_call_target="Cholesky" | custom-call | tf_op jit(solution)/shard_map/jit(cholesky)/cholesky | solution.py:49
  228.4 0.7 compare_reduce_fusion
  229.1 0.6 fusion.33
  229.8 7.9 %custom-call.32 = f32[1,103,103]{1,2,0:T(8,128)S(1)} custom-call(f32[1,103,103]{2,1,0:T(8,128)S(1)} %fusion.33), custom_call_target="InvertDiagBlocksLowerTriangular" | custom-call | tf_op jit(solution)/shard_map/jit(_cho_solve)/triangular_solve | solution.py:50
  237.7 0.2 convolution_bitcast_fusion.1
  237.8 0.2 fusion.27
  238.0 0.0 copy-done.13
  238.1 1.7 fusion.10
  239.8 0.6 add.107
  (33 shorter events, 0.2 us)
Async XLA Ops:
  0.6 16.3 %copy-start = (f32[100,4096]{1,0:T(8,128)S(1)}, f32[100,4096]{1,0:T(8,128)}, u32[]{:S(2)}) copy-start(f32[100,4096]{1,0:T(8,128)} %param.12) | copy-start | bytes 4915204
  2.1 4.2 %collective-permute-start = (f32[1]{0:T(128)}, f32[1]{0:T(128)}, u32[]{:S(2)}, u32[]{:S(2)}) collective-permute-start(f32[1]{0:T(128)} %get-tuple-element.24), channel_id=1, source_target_pairs={{0,1},{1,2},{2,3},{3,4},{4,5},{5,6},{6,7},{7,8},{8,9},{9,10},{10,1... | collective-permute-start | bytes 20 | tf_op jit(solution)/shard_map/ppermute | solution.py:13
  5.0 4.7 %collective-permute-start.1 = (f32[1]{0:T(128)}, f32[1]{0:T(128)}, u32[]{:S(2)}, u32[]{:S(2)}) collective-permute-start(f32[1]{0:T(128)} %get-tuple-element.25), channel_id=1, source_target_pairs={{1,0},{2,1},{3,2},{4,3},{5,4},{6,5},{7,6},{8,7},{9,8},{10,9},{11,1... | collective-permute-start | bytes 20 | tf_op jit(solution)/shard_map/ppermute | solution.py:13
  13.3 3.7 %copy-start.4 = (f32[4096]{0:T(1024)}, f32[4096]{0:T(1024)S(1)}, u32[]{:S(2)}) copy-start(f32[4096]{0:T(1024)S(1)} %get-tuple-element.19) | copy-start | bytes 49156
  13.3 5.1 %copy-start.2 = (f32[4096]{0:T(1024)}, f32[4096]{0:T(1024)S(1)}, u32[]{:S(2)}) copy-start(f32[4096]{0:T(1024)S(1)} %get-tuple-element.18) | copy-start | bytes 49156
  13.3 70.1 %copy-start.1 = (f32[100,4096]{1,0:T(8,128)S(1)}, f32[100,4096]{1,0:T(8,128)}, u32[]{:S(2)}) copy-start(f32[100,4096]{1,0:T(8,128)} %param.13) | copy-start | bytes 4915204
  62.4 30.4 %copy-start.6 = (f32[4096]{0:T(1024)S(1)}, f32[4096]{0:T(1024)}, u32[]{:S(2)}) copy-start(f32[4096]{0:T(1024)} %param.10) | copy-start | bytes 49156
  62.4 32.3 %copy-start.5 = (f32[4096]{0:T(1024)S(1)}, f32[4096]{0:T(1024)}, u32[]{:S(2)}) copy-start(f32[4096]{0:T(1024)} %copy-done.4) | copy-start | bytes 49156
  62.4 32.4 %copy-start.3 = (f32[4096]{0:T(1024)S(1)}, f32[4096]{0:T(1024)}, u32[]{:S(2)}) copy-start(f32[4096]{0:T(1024)} %copy-done.2) | copy-start | bytes 49156
  83.1 9.7 %copy-start.8 = (f32[4096]{0:T(1024)S(1)}, f32[4096]{0:T(1024)}, u32[]{:S(2)}) copy-start(f32[4096]{0:T(1024)} %param.11) | copy-start | bytes 49156
  85.8 3.3 %collective-permute-start.2 = (f32[1]{0:T(128)}, f32[1]{0:T(128)}, u32[]{:S(2)}, u32[]{:S(2)}) collective-permute-start(f32[1]{0:T(128)} %get-tuple-element.22), channel_id=1, source_target_pairs={{0,1},{1,2},{2,3},{3,4},{4,5},{5,6},{6,7},{7,8},{8,9},{9,10},{10,1... | collective-permute-start | bytes 20 | tf_op jit(solution)/shard_map/ppermute | solution.py:13
  87.6 5.2 %collective-permute-start.3 = (f32[1]{0:T(128)}, f32[1]{0:T(128)}, u32[]{:S(2)}, u32[]{:S(2)}) collective-permute-start(f32[1]{0:T(128)} %get-tuple-element.23), channel_id=1, source_target_pairs={{1,0},{2,1},{3,2},{4,3},{5,4},{6,5},{7,6},{8,7},{9,8},{10,9},{11,1... | collective-permute-start | bytes 20 | tf_op jit(solution)/shard_map/ppermute | solution.py:13
  94.7 2.1 copy-start.14
  94.7 3.6 %copy-start.11 = (f32[4096]{0:T(1024)}, f32[4096]{0:T(1024)S(1)}, u32[]{:S(2)}) copy-start(f32[4096]{0:T(1024)S(1)} %get-tuple-element.15) | copy-start | bytes 49156
  141.3 30.5 %copy-start.7 = (f32[4096]{0:T(1024)S(1)}, f32[4096]{0:T(1024)}, u32[]{:S(2)}) copy-start(f32[4096]{0:T(1024)} %param.10) | copy-start | bytes 49156
  141.3 30.5 %copy-start.9 = (f32[4096]{0:T(1024)S(1)}, f32[4096]{0:T(1024)}, u32[]{:S(2)}) copy-start(f32[4096]{0:T(1024)} %param.11) | copy-start | bytes 49156
  162.0 11.7 %copy-start.12 = (f32[4096]{0:T(1024)S(1)}, f32[4096]{0:T(1024)}, u32[]{:S(2)}) copy-start(f32[4096]{0:T(1024)} %copy-done.11) | copy-start | bytes 49156
  162.0 11.7 %copy-start.15 = (f32[4096]{0:T(1024)S(1)}, f32[4096]{0:T(1024)}, u32[]{:S(2)}) copy-start(f32[4096]{0:T(1024)} %copy-done.14) | copy-start | bytes 49156
  164.7 3.1 %collective-permute-start.4 = (f32[1]{0:T(128)}, f32[1]{0:T(128)}, u32[]{:S(2)}, u32[]{:S(2)}) collective-permute-start(f32[1]{0:T(128)} %get-tuple-element.20), channel_id=1, source_target_pairs={{0,1},{1,2},{2,3},{3,4},{4,5},{5,6},{6,7},{7,8},{8,9},{9,10},{10,1... | collective-permute-start | bytes 20 | tf_op jit(solution)/shard_map/ppermute | solution.py:13
  166.6 5.2 %collective-permute-start.5 = (f32[1]{0:T(128)}, f32[1]{0:T(128)}, u32[]{:S(2)}, u32[]{:S(2)}) collective-permute-start(f32[1]{0:T(128)} %get-tuple-element.21), channel_id=1, source_target_pairs={{1,0},{2,1},{3,2},{4,3},{5,4},{6,5},{7,6},{8,7},{9,8},{10,9},{11,1... | collective-permute-start | bytes 20 | tf_op jit(solution)/shard_map/ppermute | solution.py:13
  173.7 3.0 %copy-start.16 = (f32[4096]{0:T(1024)}, f32[4096]{0:T(1024)S(1)}, u32[]{:S(2)}) copy-start(f32[4096]{0:T(1024)S(1)} %get-tuple-element.11) | copy-start | bytes 49156
  175.2 62.8 %copy-start.10 = (f32[4096]{0:T(1024)S(1)}, f32[4096]{0:T(1024)}, u32[]{:S(2)}) copy-start(f32[4096]{0:T(1024)} %get-tuple-element.16) | copy-start | bytes 49156
  175.3 62.8 %copy-start.13 = (f32[4096]{0:T(1024)S(1)}, f32[4096]{0:T(1024)}, u32[]{:S(2)}) copy-start(f32[4096]{0:T(1024)} %get-tuple-element.12) | copy-start | bytes 49156
where the time goes:
time: 242 us; the launch traced here: 240 us
  blocking collectives  128 us (53%)
  other arithmetic  69.4 us (29%)
  matrix products  17.6 us (7%)
  waiting for transfers between devices  11 us (5%)
  starting transfers between devices  10.6 us (4%)
  local copies, waits for them, and re-layouts  3.08 us (1%)
    psum x3, blocking collectives, shards(): lax.psum((jnp.dot(hist_v, hist_v.T, precision=high), jnp.dot(hist_v, resi...  128 us
    another operation x9, other arithmetic, shards(): factor = jnp.linalg.cholesky(gram_matrix)  31.8 us
    another operation x6, other arithmetic, shards(): coeffs = -jax.scipy.linalg.cho_solve((factor, True), projection)  28.3 us
    ppermute x6, waiting for transfers between devices, from_behind(): lax.ppermute(value, axis, [(source, source + steps) for source in range(i...  11 us
    ppermute x6, starting transfers between devices, from_behind(): lax.ppermute(value, axis, [(source, source + steps) for source in range(i...  10.6 us
    dot_general x3, matrix products, shards(): jnp.dot(hist_v, hist_v.T, precision=high)  7.23 us
    sub x3, other arithmetic, shards(): estimate - old_estimate  6.7 us
    dot_general x3, matrix products, shards(): current = estimate + jnp.dot(coeffs, hist_w, precision=high)  5.13 us
  transfers between devices with their start and end apart: 6, of which 3 were waited for; matrix products, arithmetic and copies ran while one was open for 0% of the time, Pallas kernels for 0%

commit v1 on v0

--- a/solution.py
+++ b/solution.py
@@ -2,6 +2,7 @@
 import jax.numpy as jnp
 from jax import lax
 from jax.sharding import PartitionSpec as P
+from jax.lax import psum
 
 ITERS = 3
 coupling = 0.25
@@ -42,9 +43,15 @@
         new_column = residual - old_residual
         hist_v = jnp.concatenate([hist_v, new_column[None, :]], axis=0)
         hist_w = jnp.concatenate([hist_w, (estimate - old_estimate)[None, :]], axis=0)
-        gram_matrix, projection = lax.psum(
-            (jnp.dot(hist_v, hist_v.T, precision=high), jnp.dot(hist_v, residual, precision=high)),
-            ("iface", "dom"),
+        gram_matrix, projection = psum(
+            psum(
+                (
+                    jnp.dot(hist_v, hist_v.T, precision=high),
+                    jnp.dot(hist_v, residual, precision=high),
+                ),
+                "dom",
+            ),
+            "iface",
         )
         factor = jnp.linalg.cholesky(gram_matrix)
         coeffs = -jax.scipy.linalg.cho_solve((factor, True), projection)

time: 242 us -> 261 us (1.079)
  blocking collectives: 128 us -> 149 us
    psum x3 -> x6, blocking collectives: 128 us -> 149 us  [the longest x3 108 us: shards(): psum(psum((jnp.dot(hist_v, hist_v.T, precision=high), jnp.dot(hist_v, res...]
where the time goes in v1:
time: 261 us; the launch traced here: 259 us
  blocking collectives  149 us (57%)
  other arithmetic  69.9 us (27%)
  matrix products  17 us (7%)
  starting transfers between devices  10.4 us (4%)
  waiting for transfers between devices  8.95 us (3%)
  local copies, waits for them, and re-layouts  3.04 us (1%)
    psum x3, blocking collectives, shards(): psum(psum((jnp.dot(hist_v, hist_v.T, precision=high), jnp.dot(hist_v, res...  108 us
    psum x3, blocking collectives, shards(): psum((jnp.dot(hist_v, hist_v.T, precision=high), jnp.dot(hist_v, residual...  41.2 us
    another operation x9, other arithmetic, shards(): factor = jnp.linalg.cholesky(gram_matrix)  31.7 us
    another operation x6, other arithmetic, shards(): coeffs = -jax.scipy.linalg.cho_solve((factor, True), projection)  28.2 us
    ppermute x6, starting transfers between devices, from_behind(): lax.ppermute(value, axis, [(source, source + steps) for source in range(i...  10.4 us
    ppermute x6, waiting for transfers between devices, from_behind(): lax.ppermute(value, axis, [(source, source + steps) for source in range(i...  8.95 us
    sub x3, other arithmetic, shards(): estimate - old_estimate  7.28 us
    dot_general x3, matrix products, shards(): jnp.dot(hist_v, hist_v.T, precision=high)  6.62 us
  transfers between devices with their start and end apart: 6, of which 3 were waited for; matrix products, arithmetic and copies ran while one was open for 0% of the time, Pallas kernels for 0%

profile of v1, /device:TPU:0, one launch (start us, length us, event | category | flops | bytes accessed | tf_op | source)
XLA Modules:
  0.0 259.1 jit_solution(5965126121899318292)
XLA Ops:
  0.6 0.0 copy-start
  0.6 1.4 fusion.75
  2.1 2.9 %collective-permute-start = (f32[1]{0:T(128)}, f32[1]{0:T(128)}, u32[]{:S(2)}, u32[]{:S(2)}) collective-permute-start(f32[1]{0:T(128)} %get-tuple-element.30), channel_id=1, source_target_pairs={{0,1},{1,2},{2,3},{3,4},{4,5},{5,6},{6,7},{7,8},{8,9},{9,10},{10,1... | collective-permute-start | bytes 20 | tf_op jit(solution)/shard_map/ppermute | solution.py:14
  5.0 1.3 collective-permute-start.1
  6.3 0.0 collective-permute-done
  6.3 3.6 %collective-permute-done.1 = f32[1]{0:T(128)} collective-permute-done((f32[1]{0:T(128)}, f32[1]{0:T(128)}, u32[]{:S(2)}, u32[]{:S(2)}) %collective-permute-start.1) | collective-permute-done | bytes 36 | tf_op jit(solution)/shard_map/ppermute | solution.py:14
  9.9 2.7 %fusion.70 = (f32[4096]{0:T(1024)}, f32[4096]{0:T(1024)S(1)}) fusion(f32[4096]{0:T(1024)} %param.9, f32[1]{0:T(128)} %collective-permute-done.1, f32[4096]{0:T(1024)} %param.7, f32[1]{0:T(128)} %collective-permute-done, f32[4096]{0:T(1024)} %param.10, f32[4096]{0:T(1024)} %param.11), kind=kLoop, calls=%fused_computation.102 | loop fusion | flops 32768 | bytes 98312 | tf_op jit(solution)/shard_map/sub | solution.py:45
  12.6 0.7 fusion.72
  13.3 0.0 copy-start.1
  13.3 3.6 %fusion.19 = f32[101,101]{0,1:T(8,128)S(1)} fusion(f32[1,4096]{1,0:T(1,128)S(1)} %bitcast.102, f32[100,4096]{1,0:T(8,128)} %param.12), kind=kOutput, calls=%fused_computation.22 | convolution fusion | flops 501813248 | bytes 1695588 | tf_op jit(solution)/shard_map/dot_general | solution.py:49
  17.0 1.4 fusion.29
  18.4 14.8 %all-reduce.5 = (f32[101,101]{0,1:T(8,128)S(1)}, f32[101]{0:T(128)S(1)}) all-reduce(f32[101,101]{0,1:T(8,128)S(1)} %fusion.19, f32[101]{0:T(128)S(1)} %fusion.29), channel_id=1, replica_groups=mesh['iface'=8,'dom'=4] {'dom'}, use_global_device_ids=true, to_apply=%region_0.0 | all-reduce | flops 10302 | bytes 82416 | tf_op jit(solution)/shard_map/psum | solution.py:47
  33.2 36.0 %all-reduce.2 = (f32[101,101]{0,1:T(8,128)S(1)}, f32[101]{0:T(128)S(1)}) all-reduce(f32[101,101]{0,1:T(8,128)S(1)} %get-tuple-element.12, f32[101]{0:T(128)S(1)} %get-tuple-element.13), channel_id=1, replica_groups=mesh['iface'=8,'dom'=4] {'iface'}, use_global_device_ids=true, to_apply=%region_1.0 | all-reduce | flops 10302 | bytes 82416 | tf_op jit(solution)/shard_map/psum | solution.py:46
  69.2 0.1 copy.10
  69.3 0.6 fusion.42
  70.0 10.1 %cholesky.44 = f32[101,101]{1,0:T(8,128)S(1)} custom-call(f32[101,101]{1,0:T(8,128)} %fusion.42), custom_call_target="Cholesky" | custom-call | tf_op jit(solution)/shard_map/jit(cholesky)/cholesky | solution.py:56
  80.1 0.6 compare_reduce_fusion.2
  80.7 1.2 fusion.31
  81.9 8.5 %custom-call.30 = f32[1,101,101]{1,2,0:T(8,128)S(1)} custom-call(f32[1,101,101]{2,1,0:T(8,128)} %fusion.31), custom_call_target="InvertDiagBlocksLowerTriangular" | custom-call | tf_op jit(solution)/shard_map/jit(_cho_solve)/triangular_solve | solution.py:57
  90.4 0.2 convolution_bitcast_fusion.6
  90.6 0.2 fusion.23
  90.8 1.7 fusion
  92.5 0.6 fusion.74
  93.1 1.8 collective-permute-start.2
  94.9 1.3 collective-permute-start.3
  96.2 0.0 collective-permute-done.2
  96.2 3.3 %collective-permute-done.3 = f32[1]{0:T(128)} collective-permute-done((f32[1]{0:T(128)}, f32[1]{0:T(128)}, u32[]{:S(2)}, u32[]{:S(2)}) %collective-permute-start.3) | collective-permute-done | bytes 36 | tf_op jit(solution)/shard_map/ppermute | solution.py:14
  99.5 2.7 %fusion.67 = (f32[4096]{0:T(1024)}, f32[4096]{0:T(1024)S(1)}) fusion(f32[4096]{0:T(1024)S(1)} %get-tuple-element.23, f32[1]{0:T(128)} %collective-permute-done.3, f32[4096]{0:T(1024)S(1)} %add.109, f32[1]{0:T(128)} %collective-permute-done.2, f32[4096]{0:T(1024)} %param.10, f32[4096]{0:T(1024)} %param.11), kind=kLoop, calls=%fused_computation.100 | loop fusion | flops 32768 | bytes 98312 | tf_op jit(solution)/shard_map/sub | solution.py:45
  102.1 0.0 copy-start.9
  102.2 1.5 fusion.21
  103.7 1.4 fusion.28
  105.1 13.3 %all-reduce.4 = (f32[102,102]{0,1:T(8,128)}, f32[102]{0:T(128)S(1)}) all-reduce(f32[102,102]{0,1:T(8,128)S(1)} %fusion.21, f32[102]{0:T(128)S(1)} %fusion.28), channel_id=1, replica_groups=mesh['iface'=8,'dom'=4] {'dom'}, use_global_device_ids=true, to_apply=%region_6.7 | all-reduce | flops 10506 | bytes 84048 | tf_op jit(solution)/shard_map/psum | solution.py:47
  118.4 35.6 %all-reduce.1 = (f32[102,102]{0,1:T(8,128)S(1)}, f32[102]{0:T(128)S(1)}) all-reduce(f32[102,102]{0,1:T(8,128)} %get-tuple-element.10, f32[102]{0:T(128)S(1)} %get-tuple-element.11), channel_id=1, replica_groups=mesh['iface'=8,'dom'=4] {'iface'}, use_global_device_ids=true, to_apply=%region_7.8 | all-reduce | flops 10506 | bytes 84048 | tf_op jit(solution)/shard_map/psum | solution.py:46
  154.0 0.1 copy.12
  154.1 0.6 fusion.39
  154.7 10.2 %cholesky.86 = f32[102,102]{1,0:T(8,128)S(1)} custom-call(f32[102,102]{1,0:T(8,128)} %fusion.39), custom_call_target="Cholesky" | custom-call | tf_op jit(solution)/shard_map/jit(cholesky)/cholesky | solution.py:56
  164.9 0.7 compare_reduce_fusion.1
  165.6 1.3 fusion.32
  167.0 8.6 %custom-call.31 = f32[1,102,102]{1,2,0:T(8,128)S(1)} custom-call(f32[1,102,102]{2,1,0:T(8,128)} %fusion.32), custom_call_target="InvertDiagBlocksLowerTriangular" | custom-call | tf_op jit(solution)/shard_map/jit(_cho_solve)/triangular_solve | solution.py:57
  175.6 0.0 copy-start.10
  175.6 0.2 convolution_bitcast_fusion.4
  175.8 0.2 fusion.25
  175.9 1.7 fusion.4
  177.7 0.7 fusion.73
  178.3 1.8 collective-permute-start.4
  180.1 1.3 collective-permute-start.5
  181.4 2.1 collective-permute-done.5
  183.5 1.9 fusion.64
  185.4 0.0 copy-start.14
  185.5 1.5 fusion.30
  187.0 0.0 copy-start.8
  187.0 1.4 convolution_bitcast_fusion.2
  188.4 13.1 %all-reduce.3 = (f32[103,103]{0,1:T(8,128)S(1)}, f32[103]{0:T(128)S(1)}) all-reduce(f32[103,103]{0,1:T(8,128)S(1)} %fusion.30, f32[103]{0:T(128)S(1)} %convolution_bitcast_fusion.2), channel_id=1, replica_groups=mesh['iface'=8,'dom'=4] {'dom'}, use_global_device_ids=true, to_apply=%region_12.13 | all-reduce | flops 10712 | bytes 85696 | tf_op jit(solution)/shard_map/psum | solution.py:47
  201.5 36.1 %all-reduce = (f32[103,103]{0,1:T(8,128)S(1)}, f32[103]{0:T(128)S(1)}) all-reduce(f32[103,103]{0,1:T(8,128)S(1)} %get-tuple-element.8, f32[103]{0:T(128)S(1)} %get-tuple-element.9), channel_id=1, replica_groups=mesh['iface'=8,'dom'=4] {'iface'}, use_global_device_ids=true, to_apply=%region_13.14 | all-reduce | flops 10712 | bytes 85696 | tf_op jit(solution)/shard_map/psum | solution.py:46
  237.6 0.1 copy.14
  237.7 9.4 %cholesky.96 = f32[103,103]{1,0:T(8,128)S(1)} custom-call(f32[103,103]{1,0:T(8,128)S(1)} %fusion.36), custom_call_target="Cholesky" | custom-call | tf_op jit(solution)/shard_map/jit(cholesky)/cholesky | solution.py:56
  247.2 0.7 compare_reduce_fusion
  247.9 0.6 fusion.33
  248.5 7.9 %custom-call.32 = f32[1,103,103]{1,2,0:T(8,128)S(1)} custom-call(f32[1,103,103]{2,1,0:T(8,128)S(1)} %fusion.33), custom_call_target="InvertDiagBlocksLowerTriangular" | custom-call | tf_op jit(solution)/shard_map/jit(_cho_solve)/triangular_solve | solution.py:57
  256.4 0.2 convolution_bitcast_fusion.1
  256.6 0.2 fusion.27
  256.7 0.0 copy-done.11
  256.8 1.7 fusion.10
  258.5 0.6 add.119
  (32 shorter events, 0.2 us)
Async XLA Ops:
  0.6 16.4 %copy-start = (f32[100,4096]{1,0:T(8,128)S(1)}, f32[100,4096]{1,0:T(8,128)}, u32[]{:S(2)}) copy-start(f32[100,4096]{1,0:T(8,128)} %param.12) | copy-start | bytes 4915204
  2.1 4.2 %collective-permute-start = (f32[1]{0:T(128)}, f32[1]{0:T(128)}, u32[]{:S(2)}, u32[]{:S(2)}) collective-permute-start(f32[1]{0:T(128)} %get-tuple-element.30), channel_id=1, source_target_pairs={{0,1},{1,2},{2,3},{3,4},{4,5},{5,6},{6,7},{7,8},{8,9},{9,10},{10,1... | collective-permute-start | bytes 20 | tf_op jit(solution)/shard_map/ppermute | solution.py:14
  5.0 4.9 %collective-permute-start.1 = (f32[1]{0:T(128)}, f32[1]{0:T(128)}, u32[]{:S(2)}, u32[]{:S(2)}) collective-permute-start(f32[1]{0:T(128)} %get-tuple-element.31), channel_id=1, source_target_pairs={{1,0},{2,1},{3,2},{4,3},{5,4},{6,5},{7,6},{8,7},{9,8},{10,9},{11,1... | collective-permute-start | bytes 20 | tf_op jit(solution)/shard_map/ppermute | solution.py:14
  13.3 3.7 %copy-start.4 = (f32[4096]{0:T(1024)}, f32[4096]{0:T(1024)S(1)}, u32[]{:S(2)}) copy-start(f32[4096]{0:T(1024)S(1)} %get-tuple-element.25) | copy-start | bytes 49156
  13.3 5.1 %copy-start.2 = (f32[4096]{0:T(1024)}, f32[4096]{0:T(1024)S(1)}, u32[]{:S(2)}) copy-start(f32[4096]{0:T(1024)S(1)} %get-tuple-element.24) | copy-start | bytes 49156
  13.3 77.5 %copy-start.1 = (f32[100,4096]{1,0:T(8,128)S(1)}, f32[100,4096]{1,0:T(8,128)}, u32[]{:S(2)}) copy-start(f32[100,4096]{1,0:T(8,128)} %param.13) | copy-start | bytes 4915204
  70.0 32.1 %copy-start.5 = (f32[4096]{0:T(1024)S(1)}, f32[4096]{0:T(1024)}, u32[]{:S(2)}) copy-start(f32[4096]{0:T(1024)} %copy-done.4) | copy-start | bytes 49156
  70.0 32.2 %copy-start.3 = (f32[4096]{0:T(1024)S(1)}, f32[4096]{0:T(1024)}, u32[]{:S(2)}) copy-start(f32[4096]{0:T(1024)} %copy-done.2) | copy-start | bytes 49156
  93.1 3.1 %collective-permute-start.2 = (f32[1]{0:T(128)}, f32[1]{0:T(128)}, u32[]{:S(2)}, u32[]{:S(2)}) collective-permute-start(f32[1]{0:T(128)} %get-tuple-element.28), channel_id=1, source_target_pairs={{0,1},{1,2},{2,3},{3,4},{4,5},{5,6},{6,7},{7,8},{8,9},{9,10},{10,1... | collective-permute-start | bytes 20 | tf_op jit(solution)/shard_map/ppermute | solution.py:14
  94.9 4.6 %collective-permute-start.3 = (f32[1]{0:T(128)}, f32[1]{0:T(128)}, u32[]{:S(2)}, u32[]{:S(2)}) collective-permute-start(f32[1]{0:T(128)} %get-tuple-element.29), channel_id=1, source_target_pairs={{1,0},{2,1},{3,2},{4,3},{5,4},{6,5},{7,6},{8,7},{9,8},{10,9},{11,1... | collective-permute-start | bytes 20 | tf_op jit(solution)/shard_map/ppermute | solution.py:14
  102.1 3.0 %copy-start.9 = (f32[4096]{0:T(1024)}, f32[4096]{0:T(1024)S(1)}, u32[]{:S(2)}) copy-start(f32[4096]{0:T(1024)S(1)} %get-tuple-element.21) | copy-start | bytes 49156
  102.1 2.9 %copy-start.12 = (f32[4096]{0:T(1024)}, f32[4096]{0:T(1024)S(1)}, u32[]{:S(2)}) copy-start(f32[4096]{0:T(1024)S(1)} %get-tuple-element.20) | copy-start | bytes 49156
  154.7 28.8 %copy-start.6 = (f32[4096]{0:T(1024)S(1)}, f32[4096]{0:T(1024)}, u32[]{:S(2)}) copy-start(f32[4096]{0:T(1024)} %param.10) | copy-start | bytes 49156
  154.7 28.8 %copy-start.7 = (f32[4096]{0:T(1024)S(1)}, f32[4096]{0:T(1024)}, u32[]{:S(2)}) copy-start(f32[4096]{0:T(1024)} %param.11) | copy-start | bytes 49156
  175.6 9.8 %copy-start.10 = (f32[4096]{0:T(1024)S(1)}, f32[4096]{0:T(1024)}, u32[]{:S(2)}) copy-start(f32[4096]{0:T(1024)} %copy-done.9) | copy-start | bytes 49156
  175.6 9.9 %copy-start.13 = (f32[4096]{0:T(1024)S(1)}, f32[4096]{0:T(1024)}, u32[]{:S(2)}) copy-start(f32[4096]{0:T(1024)} %copy-done.12) | copy-start | bytes 49156
  178.3 3.1 %collective-permute-start.4 = (f32[1]{0:T(128)}, f32[1]{0:T(128)}, u32[]{:S(2)}, u32[]{:S(2)}) collective-permute-start(f32[1]{0:T(128)} %get-tuple-element.26), channel_id=1, source_target_pairs={{0,1},{1,2},{2,3},{3,4},{4,5},{5,6},{6,7},{7,8},{8,9},{9,10},{10,1... | collective-permute-start | bytes 20 | tf_op jit(solution)/shard_map/ppermute | solution.py:14
  180.1 3.4 %collective-permute-start.5 = (f32[1]{0:T(128)}, f32[1]{0:T(128)}, u32[]{:S(2)}, u32[]{:S(2)}) collective-permute-start(f32[1]{0:T(128)} %get-tuple-element.27), channel_id=1, source_target_pairs={{1,0},{2,1},{3,2},{4,3},{5,4},{6,5},{7,6},{8,7},{9,8},{10,9},{11,1... | collective-permute-start | bytes 20 | tf_op jit(solution)/shard_map/ppermute | solution.py:14
  185.4 3.0 %copy-start.14 = (f32[4096]{0:T(1024)}, f32[4096]{0:T(1024)S(1)}, u32[]{:S(2)}) copy-start(f32[4096]{0:T(1024)S(1)} %get-tuple-element.17) | copy-start | bytes 49156
  187.0 69.8 %copy-start.8 = (f32[4096]{0:T(1024)S(1)}, f32[4096]{0:T(1024)}, u32[]{:S(2)}) copy-start(f32[4096]{0:T(1024)} %get-tuple-element.22) | copy-start | bytes 49156
  187.0 69.8 %copy-start.11 = (f32[4096]{0:T(1024)S(1)}, f32[4096]{0:T(1024)}, u32[]{:S(2)}) copy-start(f32[4096]{0:T(1024)} %get-tuple-element.18) | copy-start | bytes 49156
